TPU v7x, 32 devices: a whole 2x2x4 slice. The times are simulated.
32 devices in a mesh: grp: 2 (over x), rep: 4 (over z), tp: 4 (over y, core).
Axes of the slice: x: 2, y: 2, z: 4, core: 2. Of those that a mesh axis runs over, the one named last changes fastest.
Arguments:
- grad_parts: float32 [4, 5120, 2048], P('tp', ('grp', 'rep')), may hold values from -124 to 124
- master: float32 [5120, 2048], P(('grp', 'rep'), 'tp'), may hold values from -0.078125 to 0.078125
- moment_one: float32 [5120, 2048], P(('grp', 'rep'), 'tp'), may hold values from -1.5 to 1.5
- moment_two: float32 [5120, 2048], P(('grp', 'rep'), 'tp'), may hold values from 0.003 to 0.03
- hidden_in: bfloat16 [32, 4, 5120], P(('grp', 'rep')), may hold values from -6 to 6
- queries: bfloat16 [32, 4, 5120], P(('grp', 'rep'), None, 'tp'), may hold values from -8 to 8
- cache_keys: bfloat16 [32, 1024, 1024], P(('grp', 'rep'), None, 'tp'), may hold values from -8 to 8
- cache_values: bfloat16 [32, 1024, 1024], P(('grp', 'rep'), None, 'tp'), may hold values from -6 to 6
- cache_lengths: int32 [32], P(('grp', 'rep')), may hold values from 16 to 1024
Outputs:
- new_moment_one: float32 [5120, 2048], P(('grp', 'rep'), 'tp')
- new_moment_two: float32 [5120, 2048], P(('grp', 'rep'), 'tp')
- new_entries: bfloat16 [32, 4, 2048], P(('grp', 'rep'), None, 'tp')
- attended: bfloat16 [32, 4, 5120], P(('grp', 'rep'), None, 'tp')
Inputs may be any that keep to these rules, and one draw needn't show every extreme that they name: `cache_lengths`: cache slots at or after a row's length hold no part of its cache.
All inputs are finite; a program needn't handle non-finite values.
Results may differ from a plain program's by a relative error of at most 0.0051.
Values may be sent and summed in bfloat16 or wider, within the bound.
A program may use at most 64 MiB of HBM per device.

v0:
```python
import functools
import math

import jax
import jax.numpy as jnp
from jax import lax
from jax.experimental import pallas as pl
from jax.experimental.pallas import tpu as pltpu
from jax.sharding import PartitionSpec as P

D = 5120
QH = 40
KVH = 8
HD = 128


BETA_ONE = 0.9
BETA_TWO = 0.999
FIRST_CORR = 0.9999734386011124
SECOND_CORR = 0.09520785288629041
LEARN_RATE = 0.003
EPSILON = 1e-08
ROPE_BASE = 1000000.0
NEG_FILL = -1e30


def rotate(new_keys, lengths):
    positions = (lengths[:, None] + jnp.arange(new_keys.shape[1], dtype=jnp.int32)[None, :]).astype(
        jnp.float32
    )
    half_dim = new_keys.shape[-1] // 2
    inverse = jnp.exp(
        -math.log(ROPE_BASE) * 2.0 * jnp.arange(half_dim, dtype=jnp.float32) / new_keys.shape[-1]
    )
    angles = positions[:, :, None] * inverse[None, None, :]
    cosine_part = jnp.concatenate([jnp.cos(angles), jnp.cos(angles)], -1)[:, :, None, :]
    sine_part = jnp.concatenate([jnp.sin(angles), jnp.sin(angles)], -1)[:, :, None, :]
    rotated = jnp.concatenate([-new_keys[..., half_dim:], new_keys[..., :half_dim]], -1)
    return new_keys * cosine_part + rotated * sine_part


def body(
    grad_parts,
    master,
    moment_one,
    moment_two,
    hidden_in,
    queries,
    cache_keys,
    cache_values,
    cache_lengths,
):
    col_width = master.shape[1]
    grad_sum = lax.psum_scatter(grad_parts[0], "tp", scatter_dimension=1, tiled=True)
    squares = lax.psum(jnp.sum(grad_sum * grad_sum), ("grp", "rep", "tp"))
    norm_limit = math.sqrt(D * 2 * KVH * HD)
    clipped = grad_sum * jnp.minimum(1.0, norm_limit / jnp.sqrt(squares))
    new_moment_one = BETA_ONE * moment_one + (1.0 - BETA_ONE) * clipped
    new_moment_two = BETA_TWO * moment_two + (1.0 - BETA_TWO) * clipped * clipped
    update = new_moment_one / FIRST_CORR / (jnp.sqrt(new_moment_two / SECOND_CORR) + EPSILON)
    weights = (master - LEARN_RATE * update).astype(jnp.bfloat16)
    row_count, step_count, model_width = hidden_in.shape
    token_count = row_count * step_count
    flat_inputs = hidden_in.reshape(token_count, model_width)
    sliced = lax.all_to_all(
        lax.all_to_all(flat_inputs, "grp", split_axis=1, concat_axis=0, tiled=True),
        "rep",
        split_axis=1,
        concat_axis=0,
        tiled=True,
    )
    group_count = lax.axis_size("grp")
    replica_count = lax.axis_size("rep")
    ordered = sliced.reshape(replica_count, group_count, token_count, weights.shape[0])
    ordered = jnp.swapaxes(ordered, 0, 1).reshape(
        group_count * replica_count * token_count, weights.shape[0]
    )
    projected = lax.psum_scatter(
        jnp.dot(ordered, weights, preferred_element_type=jnp.float32),
        ("grp", "rep"),
        scatter_dimension=0,
        tiled=True,
    )
    heads_here = col_width // (2 * HD)
    projected = projected.reshape(row_count, step_count, heads_here, 2, HD)
    new_keys = rotate(projected[:, :, :, 0, :], cache_lengths).astype(jnp.bfloat16)
    new_values = projected[:, :, :, 1, :].astype(jnp.bfloat16)
    new_entries = jnp.stack([new_keys, new_values], 3).reshape(row_count, step_count, col_width)
    groups = QH // KVH
    slots = cache_keys.shape[1]
    query_heads = queries.reshape(row_count, step_count, heads_here, groups, HD)
    old_k = cache_keys.reshape(row_count, slots, heads_here, HD)
    old_v = cache_values.reshape(row_count, slots, heads_here, HD)
    scaling = 1.0 / math.sqrt(HD)
    old_scores = (
        jnp.einsum("rsagd,rjad->rsagj", query_heads, old_k, preferred_element_type=jnp.float32)
        * scaling
    )
    valid_slots = jnp.arange(slots, dtype=jnp.int32)[None, :] < cache_lengths[:, None]
    old_scores = jnp.where(valid_slots[:, None, None, None, :], old_scores, NEG_FILL)
    new_scores = (
        jnp.einsum("rsagd,rtad->rsagt", query_heads, new_keys, preferred_element_type=jnp.float32)
        * scaling
    )
    causal = jnp.arange(step_count)[:, None] >= jnp.arange(step_count)[None, :]
    new_scores = jnp.where(causal[None, :, None, None, :], new_scores, NEG_FILL)
    scores = jnp.concatenate([old_scores, new_scores], -1)
    row_max = jnp.max(scores, -1, keepdims=True)
    exp_scores = jnp.exp(scores - row_max)
    probs = (exp_scores / jnp.sum(exp_scores, -1, keepdims=True)).astype(jnp.bfloat16)
    output = jnp.einsum(
        "rsagj,rjad->rsagd", probs[..., :slots], old_v, preferred_element_type=jnp.float32
    )
    output = output + jnp.einsum(
        "rsagt,rtad->rsagd", probs[..., slots:], new_values, preferred_element_type=jnp.float32
    )
    attended = output.reshape(row_count, step_count, heads_here * groups * HD).astype(jnp.bfloat16)
    return (new_moment_one, new_moment_two, new_entries, attended)


MESH = pl.DeviceIdType.MESH
CHUNK = 64
PAD = 32


def fused_kernel(
    sizes,
    lengths_ref,
    hidden_ref,
    queries_ref,
    grad_ref,
    master_ref,
    one_ref,
    two_ref,
    keys_ref,
    values_ref,
    one_out,
    two_out,
    proj_out,
    cos_out,
    sin_out,
    query_f,
    old_max,
    old_sum,
    old_out,
    lengths_s,
    queries_v,
    fwd_own,
    fwd_mate,
    sum_own,
    sum_mate,
    fwd_send,
    sum_far,
    grad_total,
    master_v,
    one_v,
    two_v,
    keys_v,
    values_v,
    hidden_in_v,
    hidden_f,
    weights_v,
    squares_send,
    squares_all,
    proj_own,
    proj_send,
    proj_recv,
    local_sem,
    mate_send_sem,
    mate_recv_sem,
    far_send_sem,
    far_recv_sem,
    hid_send_sem,
    hid_recv_sem,
    sq_send_sem,
    sq_recv_sem,
    proj_send_sem,
    proj_recv_sem,
    load_sem,
    cache_sem,
    small_sem,
    round_sem,
):
    ngrp, nrep, ntp = sizes
    ngroup = ngrp * nrep
    ndev = ngroup * ntp
    rows, cols = master_ref.shape
    nrow, nstep, width = hidden_ref.shape
    tokens = nrow * nstep
    slots = keys_ref.shape[1]
    heads = cols // (2 * HD)
    groups = QH // KVH
    nchunk = rows // CHUNK
    scaling = 1.0 / math.sqrt(HD)

    g = lax.axis_index("grp")
    r = lax.axis_index("rep")
    t = lax.axis_index("tp")
    p = g * nrep + r
    flat = p * ntp + t
    y = t // 2
    c = t % 2
    mate = y * 2 + (1 - c)
    far = (1 - y) * 2 + c
    far_mate = (1 - y) * 2 + (1 - c)

    def flat_id(k):
        f = lax.rem(flat + k, ndev)
        q = f // ntp
        return {"grp": q // nrep, "rep": lax.rem(q, nrep), "tp": lax.rem(f, ntp)}

    def group_id(k):
        q = lax.rem(p + k, ngroup)
        return {"grp": q // nrep, "rep": lax.rem(q, nrep)}

    barrier = pltpu.get_barrier_semaphore()

    bits = ndev.bit_length() - 1

    def across(b):
        stride = 1 << b
        return flat_id(ndev + stride * (1 - 2 * lax.rem(flat // stride, 2)))

    for b in range(bits):
        pl.semaphore_signal(barrier, inc=1, device_id=across(b), device_id_type=MESH)

    def block(i, owner):
        return grad_ref.at[0, pl.ds(pl.multiple_of(i * CHUNK, CHUNK), CHUNK), pl.ds(pl.multiple_of(owner * cols, cols), cols)]

    def at_rows(ref, i):
        return ref.at[pl.ds(pl.multiple_of(i * CHUNK, CHUNK), CHUNK)]

    def local_copy(which, i):
        owner, dst = ((far, fwd_own), (t, sum_own))[which]
        return pltpu.make_async_copy(block(i, owner), at_rows(dst, i), local_sem.at[which, i])

    def mate_copy(which, i):
        owner, dst = ((far_mate, fwd_mate), (mate, sum_mate))[which]
        return pltpu.make_async_remote_copy(
            src_ref=block(i, owner),
            dst_ref=at_rows(dst, i),
            send_sem=mate_send_sem.at[which, i],
            recv_sem=mate_recv_sem.at[which, i],
            device_id={"tp": mate},
            device_id_type=MESH,
        )

    def far_copy(i):
        return pltpu.make_async_remote_copy(
            src_ref=at_rows(fwd_send, i),
            dst_ref=at_rows(sum_far, i),
            send_sem=far_send_sem.at[i],
            recv_sem=far_recv_sem.at[i],
            device_id={"tp": far},
            device_id_type=MESH,
        )

    def hid_copy(k):
        q = lax.rem(p + k, ngroup)
        return pltpu.make_async_remote_copy(
            src_ref=hidden_ref.at[:, :, pl.ds(pl.multiple_of(q * rows, 128), rows)],
            dst_ref=hidden_in_v.at[k],
            send_sem=hid_send_sem.at[k - 1],
            recv_sem=hid_recv_sem.at[k - 1],
            device_id=group_id(k),
            device_id_type=MESH,
        )

    def sq_copy(k):
        return pltpu.make_async_remote_copy(
            src_ref=squares_send,
            dst_ref=squares_all.at[k],
            send_sem=sq_send_sem.at[k],
            recv_sem=sq_recv_sem.at[k],
            device_id=flat_id(k),
            device_id_type=MESH,
        )

    def proj_copy(k):
        return pltpu.make_async_remote_copy(
            src_ref=proj_send.at[k - 1],
            dst_ref=proj_recv.at[k - 1],
            send_sem=proj_send_sem.at[k - 1],
            recv_sem=proj_recv_sem.at[k - 1],
            device_id=group_id(ngroup - k),
            device_id_type=MESH,
        )

    def each(count, fn, start=0):
        def step(i, carry):
            fn(i)
            return carry

        lax.fori_loop(start, count, step, 0)

    each(nchunk, lambda i: local_copy(0, i).start())
    small = [
        pltpu.make_async_copy(src, dst, small_sem.at[i])
        for i, (src, dst) in enumerate(
            (
                (lengths_ref, lengths_s),
                (queries_ref, queries_v),
                (hidden_ref.at[:, :, pl.ds(pl.multiple_of(p * rows, 128), rows)], hidden_in_v.at[0]),
            )
        )
    ]
    for copy in small:
        copy.start()

    pl.semaphore_wait(barrier, bits)

    each(nchunk, lambda i: mate_copy(0, i).start())
    each(nchunk, lambda i: mate_copy(1, i).start())
    keys_copies = [pltpu.make_async_copy(keys_ref.at[i], keys_v.at[i], cache_sem.at[0, i]) for i in range(nrow)]
    values_copies = [pltpu.make_async_copy(values_ref.at[i], values_v.at[i], cache_sem.at[1, i]) for i in range(nrow)]
    for i in range(nrow):
        keys_copies[i].start()
        values_copies[i].start()
    each(nchunk, lambda i: local_copy(1, i).start())
    loads = [
        pltpu.make_async_copy(src, dst, load_sem.at[i])
        for i, (src, dst) in enumerate(((master_ref, master_v), (one_ref, one_v), (two_ref, two_v)))
    ]
    for copy in loads:
        copy.start()

    for copy in small:
        copy.wait()
    query_f[...] = jnp.zeros_like(query_f)
    for i in range(nrow):
        row_q = queries_v[i].astype(jnp.float32)
        for a in range(heads):
            for j in range(groups):
                n = a * groups + j
                query_f[a, i * PAD + j * nstep : i * PAD + (j + 1) * nstep, :] = row_q[:, n * HD : (n + 1) * HD]

    def forward(i):
        local_copy(0, i).wait()
        mate_copy(0, i).wait_recv()
        at_rows(fwd_send, i)[...] = (at_rows(fwd_own, i)[...] + at_rows(fwd_mate, i)[...]).astype(jnp.bfloat16)
        far_copy(i).start()

    for b in range(bits):
        pl.semaphore_signal(round_sem.at[b], inc=1, device_id=across(b), device_id_type=MESH)
        each((b + 1) * nchunk // bits, forward, b * nchunk // bits)
        pl.semaphore_wait(round_sem.at[b], 1)
    for k in range(1, ngroup):
        hid_copy(k).start()

    slot = lax.broadcasted_iota(jnp.int32, (PAD, slots), 1)
    for i in range(nrow):
        keys_copies[i].wait()
        values_copies[i].wait()
        valid = slot < lengths_s[i]
        for a in range(heads):
            q = query_f[a, i * PAD : (i + 1) * PAD, :].astype(jnp.bfloat16)
            scores = lax.dot_general(
                q,
                keys_v[i, :, a * HD : (a + 1) * HD],
                (((1,), (1,)), ((), ())),
                preferred_element_type=jnp.float32,
            )
            scores = jnp.where(valid, scores * scaling, NEG_FILL)
            top = jnp.max(scores, -1, keepdims=True)
            e = jnp.exp(scores - top)
            here = slice(i * PAD, (i + 1) * PAD)
            old_max[a, here, :] = jnp.broadcast_to(top, (PAD, HD))
            old_sum[a, here, :] = jnp.broadcast_to(jnp.sum(e, -1, keepdims=True), (PAD, HD))
            old_out[a, here, :] = jnp.dot(
                e.astype(jnp.bfloat16), values_v[i, :, a * HD : (a + 1) * HD], preferred_element_type=jnp.float32
            )

    for k in range(ngroup):
        if k > 0:
            hid_copy(k).wait_recv()
        own = hidden_in_v[k]
        for i in range(nrow):
            at = k * tokens + i * nstep
            hidden_f[at : at + nstep, :] = own[i].astype(jnp.float32)

    token = lax.broadcasted_iota(jnp.int32, (tokens, HD), 0)
    lane = lax.broadcasted_iota(jnp.int32, (tokens, HD), 1)
    position = lax.rem(token, nstep)
    for i in range(nrow):
        position = position + jnp.where(token // nstep == i, lengths_s[i], 0)
    pair = lax.rem(lane, HD // 2).astype(jnp.float32)
    angle = position.astype(jnp.float32) * jnp.exp(-math.log(ROPE_BASE) * 2.0 * pair / HD)
    cos_out[...] = jnp.cos(angle)
    sin_out[...] = jnp.where(lane < HD // 2, -jnp.sin(angle), jnp.sin(angle))

    def total(i, acc):
        local_copy(1, i).wait()
        mate_copy(1, i).wait_recv()
        far_copy(i).wait_recv()
        s = at_rows(sum_own, i)[...] + at_rows(sum_mate, i)[...] + at_rows(sum_far, i)[...].astype(jnp.float32)
        at_rows(grad_total, i)[...] = s
        return acc + jnp.sum((s * s).reshape(CHUNK // 8, 8, cols), axis=0)

    acc = lax.fori_loop(0, nchunk, total, jnp.zeros((8, cols), jnp.float32))
    part = jnp.sum(acc, axis=0, keepdims=True)
    mine = sum(part[:, j * 128 : (j + 1) * 128] for j in range(cols // 128))
    squares_send[...] = mine
    each(ndev, lambda k: sq_copy(k).start(), 1)
    squares_all[0] = mine
    for copy in loads:
        copy.wait()
    each(ndev, lambda k: sq_copy(k).wait_recv(), 1)
    squares = jnp.sum(jnp.sum(squares_all[...], axis=0), axis=1, keepdims=True)
    norm_limit = math.sqrt(D * 2 * KVH * HD)
    factor = jnp.minimum(1.0, norm_limit / jnp.sqrt(jnp.broadcast_to(squares, (1, cols))))

    def adam(i):
        clipped = at_rows(grad_total, i)[...] * factor
        one = BETA_ONE * at_rows(one_v, i)[...] + (1.0 - BETA_ONE) * clipped
        two = BETA_TWO * at_rows(two_v, i)[...] + (1.0 - BETA_TWO) * clipped * clipped
        at_rows(one_out, i)[...] = one
        at_rows(two_out, i)[...] = two
        update = (one * (LEARN_RATE / FIRST_CORR)) / (jnp.sqrt(two * (1.0 / SECOND_CORR)) + EPSILON)
        at_rows(weights_v, i)[...] = (at_rows(master_v, i)[...] - update).astype(jnp.bfloat16)

    each(nchunk, adam)
    partial = jnp.dot(hidden_f[...].astype(jnp.bfloat16), weights_v[...], preferred_element_type=jnp.float32)
    for k in range(1, ngroup):
        proj_send[k - 1] = partial[k * tokens : (k + 1) * tokens].astype(jnp.bfloat16)
        proj_copy(k).start()
    proj_own[...] = partial[0:tokens]

    each(nchunk, lambda i: mate_copy(0, i).wait_send())
    each(nchunk, lambda i: mate_copy(1, i).wait_send())
    each(nchunk, lambda i: far_copy(i).wait_send())
    each(ndev, lambda k: sq_copy(k).wait_send(), 1)
    for k in range(1, ngroup):
        hid_copy(k).wait_send()

    projected = proj_own[...]
    for k in range(1, ngroup):
        proj_copy(k).wait_recv()
        projected = projected + proj_recv[k - 1].astype(jnp.float32)
    proj_out[...] = projected
    for k in range(1, ngroup):
        proj_copy(k).wait_send()


def finish_kernel(
    one_ref,
    two_ref,
    proj_ref,
    cos_ref,
    sin_ref,
    query_ref,
    max_ref,
    sum_ref,
    old_ref,
    one_out,
    two_out,
    entries_out,
    attended_out,
    heads_v,
    out_sem,
):
    outs = [
        pltpu.make_async_copy(one_ref, one_out, out_sem.at[0]),
        pltpu.make_async_copy(two_ref, two_out, out_sem.at[1]),
    ]
    for copy in outs:
        copy.start()
    nrow, nstep, cols = entries_out.shape
    tokens = nrow * nstep
    heads = cols // (2 * HD)
    groups = QH // KVH
    scaling = 1.0 / math.sqrt(HD)
    qi = lax.broadcasted_iota(jnp.int32, (nrow * PAD, tokens), 0)
    kj = lax.broadcasted_iota(jnp.int32, (nrow * PAD, tokens), 1)
    seen = (qi // PAD == kj // nstep) & (qi % nstep >= kj % nstep)
    for a in range(heads):
        k = proj_ref[:, 2 * a * HD : (2 * a + 1) * HD]
        k = k * cos_ref[...] + pltpu.roll(k, HD // 2, 1) * sin_ref[...]
        v = proj_ref[:, (2 * a + 1) * HD : (2 * a + 2) * HD]
        new_k = k.astype(jnp.bfloat16)
        new_v = v.astype(jnp.bfloat16)
        for i in range(nrow):
            rows_i = slice(i * nstep, (i + 1) * nstep)
            entries_out[i, :, 2 * a * HD : (2 * a + 1) * HD] = k[rows_i].astype(jnp.bfloat16)
            entries_out[i, :, (2 * a + 1) * HD : (2 * a + 2) * HD] = v[rows_i].astype(jnp.bfloat16)
        scores = lax.dot_general(
            query_ref[a].astype(jnp.bfloat16), new_k, (((1,), (1,)), ((), ())), preferred_element_type=jnp.float32
        )
        scores = jnp.where(seen, scores * scaling, NEG_FILL)
        before = max_ref[a][:, 0:1]
        top = jnp.maximum(before, jnp.max(scores, -1, keepdims=True))
        alpha = jnp.exp(before - top)
        e = jnp.exp(scores - top)
        whole = sum_ref[a][:, 0:1] * alpha + jnp.sum(e, -1, keepdims=True)
        o = old_ref[a] * alpha + jnp.dot(e.astype(jnp.bfloat16), new_v, preferred_element_type=jnp.float32)
        heads_v[a] = o / whole
        for i in range(nrow):
            for j in range(groups):
                n = a * groups + j
                at = i * PAD + j * nstep
                attended_out[i, :, n * HD : (n + 1) * HD] = heads_v[a, at : at + nstep, :].astype(jnp.bfloat16)
    for copy in outs:
        copy.wait()


def fused_body(
    sizes,
    grad_parts,
    master,
    moment_one,
    moment_two,
    hidden_in,
    queries,
    cache_keys,
    cache_values,
    cache_lengths,
):
    ngrp, nrep, ntp = sizes
    ngroup = ngrp * nrep
    ndev = ngroup * ntp
    rows, cols = master.shape
    nrow, nstep, width = hidden_in.shape
    tokens = nrow * nstep
    heads = cols // (2 * HD)
    nchunk = rows // CHUNK
    f32, bf16 = jnp.float32, jnp.bfloat16
    vm = pltpu.VMEM
    dma = pltpu.SemaphoreType.DMA
    vmem = pl.BlockSpec(memory_space=pltpu.VMEM)
    hbm = pl.BlockSpec(memory_space=pltpu.HBM)
    per_head = vm((heads, nrow * PAD, HD), f32)
    moment = vm((rows, cols), f32)
    table = vm((tokens, HD), f32)
    middle = pl.pallas_call(
        functools.partial(fused_kernel, sizes),
        out_shape=(moment, moment, vm((tokens, cols), f32), table, table) + (per_head,) * 4,
        in_specs=[hbm] * 9,
        out_specs=(vmem,) * 9,
        scratch_shapes=[
            pltpu.SMEM((nrow,), jnp.int32),
            vm(queries.shape, bf16),
            vm((rows, cols), f32),
            vm((rows, cols), f32),
            vm((rows, cols), f32),
            vm((rows, cols), f32),
            vm((rows, cols), bf16),
            vm((rows, cols), bf16),
            vm((rows, cols), f32),
            vm((rows, cols), f32),
            vm((rows, cols), f32),
            vm((rows, cols), f32),
            vm(cache_keys.shape, bf16),
            vm(cache_values.shape, bf16),
            vm((ngroup, nrow, nstep, rows), bf16),
            vm((ngroup * tokens, rows), f32),
            vm((rows, cols), bf16),
            vm((1, 128), f32),
            vm((ndev, 1, 128), f32),
            vm((tokens, cols), f32),
            vm((ngroup - 1, tokens, cols), bf16),
            vm((ngroup - 1, tokens, cols), bf16),
            dma((2, nchunk)),
            dma((2, nchunk)),
            dma((2, nchunk)),
            dma((nchunk,)),
            dma((nchunk,)),
            dma((ngroup - 1,)),
            dma((ngroup - 1,)),
            dma((ndev,)),
            dma((ndev,)),
            dma((ngroup - 1,)),
            dma((ngroup - 1,)),
            dma((3,)),
            dma((2, nrow)),
            dma((3,)),
            pltpu.SemaphoreType.REGULAR((ndev.bit_length() - 1,)),
        ],
        compiler_params=pltpu.CompilerParams(
            collective_id=0, has_side_effects=True, vmem_limit_bytes=60 * 1024 * 1024 + 320 * 1024
        ),
    )(cache_lengths, hidden_in, queries, grad_parts, master, moment_one, moment_two, cache_keys, cache_values)
    return pl.pallas_call(
        finish_kernel,
        out_shape=(
            jax.ShapeDtypeStruct((rows, cols), f32),
            jax.ShapeDtypeStruct((rows, cols), f32),
            jax.ShapeDtypeStruct((nrow, nstep, cols), bf16),
            jax.ShapeDtypeStruct(queries.shape, bf16),
        ),
        in_specs=[vmem] * 9,
        out_specs=(hbm, hbm, vmem, vmem),
        scratch_shapes=[vm((heads, nrow * PAD, HD), f32), dma((2,))],
        compiler_params=pltpu.CompilerParams(vmem_limit_bytes=8 * 1024 * 1024),
    )(*middle)


def solution(mesh):
    sizes = (mesh.shape["grp"], mesh.shape["rep"], mesh.shape["tp"])
    fits = sizes[2] == 4 and D % (sizes[0] * sizes[1] * 128) == 0 and KVH % sizes[2] == 0
    fits = fits and (sizes[0] * sizes[1]) & (sizes[0] * sizes[1] - 1) == 0
    placed = (
        P("tp", ("grp", "rep"), None),
        P(("grp", "rep"), "tp"),
        P(("grp", "rep"), "tp"),
        P(("grp", "rep"), "tp"),
        P(("grp", "rep"), None, None),
        P(("grp", "rep"), None, "tp"),
        P(("grp", "rep"), None, "tp"),
        P(("grp", "rep"), None, "tp"),
        P(("grp", "rep")),
    )
    return jax.shard_map(
        functools.partial(fused_body, sizes) if fits else body,
        mesh=mesh,
        in_specs=placed,
        out_specs=(
            P(("grp", "rep"), "tp"),
            P(("grp", "rep"), "tp"),
            P(("grp", "rep"), None, "tp"),
            P(("grp", "rep"), None, "tp"),
        ),
        check_vma=False,
    )
```

profile of v0, /device:TPU:0, one launch (start us, length us, event | category | flops | bytes accessed | tf_op | source)
XLA Modules:
  0.0 37.7 jit_solution(8623157536725170450)
XLA Ops:
  0.6 35.0 %shard_map.120 = (f32[640,512]{1,0:T(8,128)S(1)}, f32[640,512]{1,0:T(8,128)S(1)}, f32[16,512]{1,0:T(8,128)S(1)}, f32[16,128]{1,0:T(8,128)S(1)}, f32[16,128]{1,0:...) custom-call(s32[4]{0:T(128)} %lengths_ref.1, ...), custom_call_target="tpu_custom_call" | custom-call | tf_op jit(solution)/shard_map/pallas_call | solution.py:533
  35.6 2.1 %shard_map.121 = (f32[640,512]{1,0:T(8,128)}, f32[640,512]{1,0:T(8,128)}, bf16[4,4,512]{2,1,0:T(4,128)(2,1)}, bf16[4,4,1280]{2,1,0:T(4,128)(2,1)}) custom-call(f32[640,512]{1,0:T(8,128)S(1)} %get-tuple-element.13.one_ref, f32[640,512]{1,0:T(8,128)S(1)} %get-tuple-element.14.two_ref, f32[16,512]{1,0:T(8,128)S(1)} %get-tuple-element.15.proj_ref, ...), custom_call_target="tpu_custom_call" | custom-call | tf_op jit(solution)/shard_map/pallas_call | solution.py:581
where the time goes:
time: 37.9 us; the launch traced here: 37.7 us
  Pallas kernels  37.1 us (98%)
  between operations  0.64 us (2%)
    pallas_call x1, Pallas kernels, fused_body(): pl.pallas_call(functools.partial(fused_kernel, sizes), out_shape=(moment,...  35 us
    pallas_call x1, Pallas kernels, fused_body(): pl.pallas_call(finish_kernel, out_shape=(jax.ShapeDtypeStruct((rows, cols...  2.13 us

commit v1 on v0

--- a/solution.py
+++ b/solution.py
@@ -119,8 +119,19 @@
 
 
 MESH = pl.DeviceIdType.MESH
-CHUNK = 64
 PAD = 32
+BLOCK = 128
+EARLY = 2
+
+
+def chunk_plan(rows):
+    sizes = [32, 64]
+    left = rows - sum(sizes) - 32
+    while left > 0:
+        sizes.append(min(96, left))
+        left -= sizes[-1]
+    sizes.append(32)
+    return [(sum(sizes[:i]), n) for i, n in enumerate(sizes)]
 
 
 def fused_kernel(
@@ -145,40 +156,40 @@
     old_out,
     lengths_s,
     queries_v,
-    fwd_own,
-    fwd_mate,
-    sum_own,
-    sum_mate,
+    mate_src,
+    fwd_in,
     fwd_send,
     sum_far,
+    sum_in,
     grad_total,
-    master_v,
-    one_v,
-    two_v,
-    keys_v,
-    values_v,
+    state_v,
+    cache_v,
     hidden_in_v,
     hidden_f,
+    hidden_b,
     weights_v,
     squares_send,
     squares_all,
     proj_own,
     proj_send,
     proj_recv,
-    local_sem,
+    fwd_sem,
+    far_recv_sem,
+    proj_recv_sem,
+    cache_sem,
+    sum_sem,
+    early_sem,
     mate_send_sem,
-    mate_recv_sem,
     far_send_sem,
-    far_recv_sem,
     hid_send_sem,
     hid_recv_sem,
     sq_send_sem,
     sq_recv_sem,
     proj_send_sem,
-    proj_recv_sem,
     load_sem,
-    cache_sem,
-    small_sem,
+    length_sem,
+    query_sem,
+    own_sem,
     round_sem,
 ):
     ngrp, nrep, ntp = sizes
@@ -190,79 +201,103 @@
     slots = keys_ref.shape[1]
     heads = cols // (2 * HD)
     groups = QH // KVH
-    nchunk = rows // CHUNK
+    plan = chunk_plan(rows)
+    nchunk = len(plan)
+    nblock = cols // BLOCK
     scaling = 1.0 / math.sqrt(HD)
 
     g = lax.axis_index("grp")
     r = lax.axis_index("rep")
     t = lax.axis_index("tp")
     p = g * nrep + r
-    flat = p * ntp + t
     y = t // 2
     c = t % 2
     mate = y * 2 + (1 - c)
     far = (1 - y) * 2 + c
     far_mate = (1 - y) * 2 + (1 - c)
 
-    def flat_id(k):
-        f = lax.rem(flat + k, ndev)
-        q = f // ntp
-        return {"grp": q // nrep, "rep": lax.rem(q, nrep), "tp": lax.rem(f, ntp)}
-
-    def group_id(k):
-        q = lax.rem(p + k, ngroup)
-        return {"grp": q // nrep, "rep": lax.rem(q, nrep)}
+    def toggles(v, size):
+        return [(1 << b) * (1 - 2 * lax.rem(lax.div(v, 1 << b), 2)) for b in range(size.bit_length() - 1)]
+
+    flips = {"grp": toggles(g, ngrp), "rep": toggles(r, nrep), "tp": toggles(t, ntp)}
+    base = {"grp": g, "rep": r, "tp": t}
+
+    def peer(**bits):
+        return {
+            name: base[name] + sum(d for b, d in enumerate(flips[name]) if bits.get(name, 0) >> b & 1)
+            for name in base
+        }
+
+    def group_bits(k):
+        return {"grp": k // nrep, "rep": k % nrep}
+
+    def group_peer(k):
+        return peer(**group_bits(k))
+
+    def flat_bits(k):
+        return {"tp": k % ntp, **group_bits(k // ntp)}
+
+    def hops(k):
+        bits = flat_bits(k)
+        return bits["grp"] + bits["rep"] + bits["tp"] // 2 + 0.3 * (bits["tp"] % 2)
+
+    flat_order = sorted(range(1, ndev), key=hops, reverse=True)
+    group_order = sorted(range(1, ngroup), key=lambda k: hops(k * ntp), reverse=True)
 
     barrier = pltpu.get_barrier_semaphore()
-
     bits = ndev.bit_length() - 1
 
     def across(b):
-        stride = 1 << b
-        return flat_id(ndev + stride * (1 - 2 * lax.rem(flat // stride, 2)))
+        return peer(**flat_bits(1 << b))
 
     for b in range(bits):
         pl.semaphore_signal(barrier, inc=1, device_id=across(b), device_id_type=MESH)
 
-    def block(i, owner):
-        return grad_ref.at[0, pl.ds(pl.multiple_of(i * CHUNK, CHUNK), CHUNK), pl.ds(pl.multiple_of(owner * cols, cols), cols)]
-
-    def at_rows(ref, i):
-        return ref.at[pl.ds(pl.multiple_of(i * CHUNK, CHUNK), CHUNK)]
-
-    def local_copy(which, i):
-        owner, dst = ((far, fwd_own), (t, sum_own))[which]
-        return pltpu.make_async_copy(block(i, owner), at_rows(dst, i), local_sem.at[which, i])
-
-    def mate_copy(which, i):
-        owner, dst = ((far_mate, fwd_mate), (mate, sum_mate))[which]
+    def block(start, n, owner):
+        return grad_ref.at[0, pl.ds(start, n), pl.ds(pl.multiple_of(owner * cols, cols), cols)]
+
+    def drain(ref, sem):
+        pltpu.make_async_copy(ref, ref, sem).wait()
+
+    early = sum(n for _, n in plan[:EARLY])
+    early_copy = pltpu.make_async_copy(block(0, early, far_mate), mate_src, early_sem)
+    early_copy.start()
+
+    def own_copy(i):
+        start, n = plan[i]
+        return pltpu.make_async_copy(block(start, n, far), fwd_in.at[pl.ds(2 * start, n)], fwd_sem.at[i])
+
+    def mate_copy(i):
+        start, n = plan[i]
         return pltpu.make_async_remote_copy(
-            src_ref=block(i, owner),
-            dst_ref=at_rows(dst, i),
-            send_sem=mate_send_sem.at[which, i],
-            recv_sem=mate_recv_sem.at[which, i],
-            device_id={"tp": mate},
+            src_ref=mate_src.at[pl.ds(start, n)] if i < EARLY else block(start, n, far_mate),
+            dst_ref=fwd_in.at[pl.ds(2 * start + n, n)],
+            send_sem=mate_send_sem,
+            recv_sem=fwd_sem.at[i],
+            device_id=peer(tp=1),
             device_id_type=MESH,
         )
 
     def far_copy(i):
+        start, n = plan[i]
         return pltpu.make_async_remote_copy(
-            src_ref=at_rows(fwd_send, i),
-            dst_ref=at_rows(sum_far, i),
-            send_sem=far_send_sem.at[i],
+            src_ref=fwd_send.at[pl.ds(start, n)],
+            dst_ref=sum_far.at[pl.ds(start, n)],
+            send_sem=far_send_sem,
             recv_sem=far_recv_sem.at[i],
-            device_id={"tp": far},
+            device_id=peer(tp=2),
             device_id_type=MESH,
         )
 
     def hid_copy(k):
-        q = lax.rem(p + k, ngroup)
+        to = group_peer(k)
+        q = to["grp"] * nrep + to["rep"]
         return pltpu.make_async_remote_copy(
             src_ref=hidden_ref.at[:, :, pl.ds(pl.multiple_of(q * rows, 128), rows)],
             dst_ref=hidden_in_v.at[k],
-            send_sem=hid_send_sem.at[k - 1],
-            recv_sem=hid_recv_sem.at[k - 1],
-            device_id=group_id(k),
+            send_sem=hid_send_sem,
+            recv_sem=hid_recv_sem,
+            device_id=to,
             device_id_type=MESH,
         )
 
@@ -270,61 +305,69 @@
         return pltpu.make_async_remote_copy(
             src_ref=squares_send,
             dst_ref=squares_all.at[k],
-            send_sem=sq_send_sem.at[k],
-            recv_sem=sq_recv_sem.at[k],
-            device_id=flat_id(k),
+            send_sem=sq_send_sem,
+            recv_sem=sq_recv_sem,
+            device_id=peer(**flat_bits(k)),
             device_id_type=MESH,
         )
 
-    def proj_copy(k):
+    def proj_copy(j, k):
         return pltpu.make_async_remote_copy(
-            src_ref=proj_send.at[k - 1],
-            dst_ref=proj_recv.at[k - 1],
-            send_sem=proj_send_sem.at[k - 1],
-            recv_sem=proj_recv_sem.at[k - 1],
-            device_id=group_id(ngroup - k),
+            src_ref=proj_send.at[j, k - 1],
+            dst_ref=proj_recv.at[j, k - 1],
+            send_sem=proj_send_sem,
+            recv_sem=proj_recv_sem.at[j],
+            device_id=group_peer(k),
             device_id_type=MESH,
         )
 
-    def each(count, fn, start=0):
-        def step(i, carry):
-            fn(i)
-            return carry
-
-        lax.fori_loop(start, count, step, 0)
-
-    each(nchunk, lambda i: local_copy(0, i).start())
-    small = [
-        pltpu.make_async_copy(src, dst, small_sem.at[i])
-        for i, (src, dst) in enumerate(
-            (
-                (lengths_ref, lengths_s),
-                (queries_ref, queries_v),
-                (hidden_ref.at[:, :, pl.ds(pl.multiple_of(p * rows, 128), rows)], hidden_in_v.at[0]),
-            )
-        )
-    ]
-    for copy in small:
+    for i in range(nchunk):
+        own_copy(i).start()
+    length_copy = pltpu.make_async_copy(lengths_ref, lengths_s, length_sem)
+    query_copy = pltpu.make_async_copy(queries_ref, queries_v, query_sem)
+    own_hidden = pltpu.make_async_copy(
+        hidden_ref.at[:, :, pl.ds(pl.multiple_of(p * rows, 128), rows)], hidden_in_v.at[0], own_sem
+    )
+    for copy in (length_copy, query_copy, own_hidden):
         copy.start()
 
+    early_copy.wait()
     pl.semaphore_wait(barrier, bits)
 
-    each(nchunk, lambda i: mate_copy(0, i).start())
-    each(nchunk, lambda i: mate_copy(1, i).start())
-    keys_copies = [pltpu.make_async_copy(keys_ref.at[i], keys_v.at[i], cache_sem.at[0, i]) for i in range(nrow)]
-    values_copies = [pltpu.make_async_copy(values_ref.at[i], values_v.at[i], cache_sem.at[1, i]) for i in range(nrow)]
+    for i in range(nchunk):
+        mate_copy(i).start()
+    pltpu.make_async_remote_copy(
+        src_ref=block(0, rows, mate),
+        dst_ref=sum_in.at[1],
+        send_sem=mate_send_sem,
+        recv_sem=sum_sem,
+        device_id=peer(tp=1),
+        device_id_type=MESH,
+    ).start()
     for i in range(nrow):
-        keys_copies[i].start()
-        values_copies[i].start()
-    each(nchunk, lambda i: local_copy(1, i).start())
-    loads = [
-        pltpu.make_async_copy(src, dst, load_sem.at[i])
-        for i, (src, dst) in enumerate(((master_ref, master_v), (one_ref, one_v), (two_ref, two_v)))
-    ]
-    for copy in loads:
-        copy.start()
-
-    for copy in small:
+        pltpu.make_async_copy(keys_ref.at[i], cache_v.at[i, 0], cache_sem.at[i]).start()
+        pltpu.make_async_copy(values_ref.at[i], cache_v.at[i, 1], cache_sem.at[i]).start()
+    pltpu.make_async_copy(block(0, rows, t), sum_in.at[0], sum_sem).start()
+    for i, src in enumerate((one_ref, two_ref, master_ref)):
+        pltpu.make_async_copy(src, state_v.at[i], load_sem).start()
+
+    def forward(i):
+        start, n = plan[i]
+        drain(fwd_in.at[pl.ds(2 * start, 2 * n)], fwd_sem.at[i])
+        fwd_send[start : start + n, :] = (
+            fwd_in[2 * start : 2 * start + n, :] + fwd_in[2 * start + n : 2 * start + 2 * n, :]
+        ).astype(jnp.bfloat16)
+        far_copy(i).start()
+
+    for b in range(bits):
+        pl.semaphore_signal(round_sem.at[b], inc=1, device_id=across(b), device_id_type=MESH)
+        for i in range(b * nchunk // bits, (b + 1) * nchunk // bits):
+            forward(i)
+        pl.semaphore_wait(round_sem.at[b], 1)
+    for k in group_order:
+        hid_copy(k).start()
+
+    for copy in (length_copy, query_copy):
         copy.wait()
     query_f[...] = jnp.zeros_like(query_f)
     for i in range(nrow):
@@ -334,29 +377,15 @@
                 n = a * groups + j
                 query_f[a, i * PAD + j * nstep : i * PAD + (j + 1) * nstep, :] = row_q[:, n * HD : (n + 1) * HD]
 
-    def forward(i):
-        local_copy(0, i).wait()
-        mate_copy(0, i).wait_recv()
-        at_rows(fwd_send, i)[...] = (at_rows(fwd_own, i)[...] + at_rows(fwd_mate, i)[...]).astype(jnp.bfloat16)
-        far_copy(i).start()
-
-    for b in range(bits):
-        pl.semaphore_signal(round_sem.at[b], inc=1, device_id=across(b), device_id_type=MESH)
-        each((b + 1) * nchunk // bits, forward, b * nchunk // bits)
-        pl.semaphore_wait(round_sem.at[b], 1)
-    for k in range(1, ngroup):
-        hid_copy(k).start()
-
     slot = lax.broadcasted_iota(jnp.int32, (PAD, slots), 1)
     for i in range(nrow):
-        keys_copies[i].wait()
-        values_copies[i].wait()
+        drain(cache_v.at[i], cache_sem.at[i])
         valid = slot < lengths_s[i]
         for a in range(heads):
             q = query_f[a, i * PAD : (i + 1) * PAD, :].astype(jnp.bfloat16)
             scores = lax.dot_general(
                 q,
-                keys_v[i, :, a * HD : (a + 1) * HD],
+                cache_v[i, 0, :, a * HD : (a + 1) * HD],
                 (((1,), (1,)), ((), ())),
                 preferred_element_type=jnp.float32,
             )
@@ -367,16 +396,8 @@
             old_max[a, here, :] = jnp.broadcast_to(top, (PAD, HD))
             old_sum[a, here, :] = jnp.broadcast_to(jnp.sum(e, -1, keepdims=True), (PAD, HD))
             old_out[a, here, :] = jnp.dot(
-                e.astype(jnp.bfloat16), values_v[i, :, a * HD : (a + 1) * HD], preferred_element_type=jnp.float32
+                e.astype(jnp.bfloat16), cache_v[i, 1, :, a * HD : (a + 1) * HD], preferred_element_type=jnp.float32
             )
-
-    for k in range(ngroup):
-        if k > 0:
-            hid_copy(k).wait_recv()
-        own = hidden_in_v[k]
-        for i in range(nrow):
-            at = k * tokens + i * nstep
-            hidden_f[at : at + nstep, :] = own[i].astype(jnp.float32)
 
     token = lax.broadcasted_iota(jnp.int32, (tokens, HD), 0)
     lane = lax.broadcasted_iota(jnp.int32, (tokens, HD), 1)
@@ -388,57 +409,74 @@
     cos_out[...] = jnp.cos(angle)
     sin_out[...] = jnp.where(lane < HD // 2, -jnp.sin(angle), jnp.sin(angle))
 
-    def total(i, acc):
-        local_copy(1, i).wait()
-        mate_copy(1, i).wait_recv()
-        far_copy(i).wait_recv()
-        s = at_rows(sum_own, i)[...] + at_rows(sum_mate, i)[...] + at_rows(sum_far, i)[...].astype(jnp.float32)
-        at_rows(grad_total, i)[...] = s
-        return acc + jnp.sum((s * s).reshape(CHUNK // 8, 8, cols), axis=0)
-
-    acc = lax.fori_loop(0, nchunk, total, jnp.zeros((8, cols), jnp.float32))
-    part = jnp.sum(acc, axis=0, keepdims=True)
-    mine = sum(part[:, j * 128 : (j + 1) * 128] for j in range(cols // 128))
+    drain(state_v, load_sem)
+
+    def prescale(i, carry):
+        here = pl.ds(pl.multiple_of(i * 64, 64), 64)
+        state_v[0, here, :] = BETA_ONE * state_v[0, here, :]
+        state_v[1, here, :] = BETA_TWO * state_v[1, here, :]
+        return carry
+
+    lax.fori_loop(0, rows // 64, prescale, 0)
+
+    own_hidden.wait()
+    drain(hidden_in_v.at[pl.ds(1, ngroup - 1)], hid_recv_sem)
+    for k in range(ngroup):
+        own = hidden_in_v[k]
+        for i in range(nrow):
+            at = k * tokens + i * nstep
+            hidden_f[at : at + nstep, :] = own[i].astype(jnp.float32)
+    hidden_b[...] = hidden_f[...].astype(jnp.bfloat16)
+
+    drain(sum_in, sum_sem)
+    acc = jnp.zeros((8, cols), jnp.float32)
+    for i, (start, n) in enumerate(plan):
+        here = slice(start, start + n)
+        drain(sum_far.at[pl.ds(start, n)], far_recv_sem.at[i])
+        s = sum_in[0, here, :] + sum_in[1, here, :] + sum_far[here, :].astype(jnp.float32)
+        grad_total[here, :] = s
+        acc = acc + jnp.sum((s * s).reshape(n // 8, 8, cols), axis=0)
+    mine = jnp.sum(sum(acc[:, j * 128 : (j + 1) * 128] for j in range(cols // 128)), axis=0, keepdims=True)
     squares_send[...] = mine
-    each(ndev, lambda k: sq_copy(k).start(), 1)
+    for k in flat_order:
+        sq_copy(k).start()
     squares_all[0] = mine
-    for copy in loads:
-        copy.wait()
-    each(ndev, lambda k: sq_copy(k).wait_recv(), 1)
+    drain(fwd_in, mate_send_sem)
+    drain(fwd_send, far_send_sem)
+    drain(hidden_in_v.at[pl.ds(1, ngroup - 1)], hid_send_sem)
+    drain(squares_all.at[pl.ds(1, ndev - 1)], sq_recv_sem)
     squares = jnp.sum(jnp.sum(squares_all[...], axis=0), axis=1, keepdims=True)
     norm_limit = math.sqrt(D * 2 * KVH * HD)
-    factor = jnp.minimum(1.0, norm_limit / jnp.sqrt(jnp.broadcast_to(squares, (1, cols))))
-
-    def adam(i):
-        clipped = at_rows(grad_total, i)[...] * factor
-        one = BETA_ONE * at_rows(one_v, i)[...] + (1.0 - BETA_ONE) * clipped
-        two = BETA_TWO * at_rows(two_v, i)[...] + (1.0 - BETA_TWO) * clipped * clipped
-        at_rows(one_out, i)[...] = one
-        at_rows(two_out, i)[...] = two
-        update = (one * (LEARN_RATE / FIRST_CORR)) / (jnp.sqrt(two * (1.0 / SECOND_CORR)) + EPSILON)
-        at_rows(weights_v, i)[...] = (at_rows(master_v, i)[...] - update).astype(jnp.bfloat16)
-
-    each(nchunk, adam)
-    partial = jnp.dot(hidden_f[...].astype(jnp.bfloat16), weights_v[...], preferred_element_type=jnp.float32)
-    for k in range(1, ngroup):
-        proj_send[k - 1] = partial[k * tokens : (k + 1) * tokens].astype(jnp.bfloat16)
-        proj_copy(k).start()
-    proj_own[...] = partial[0:tokens]
-
-    each(nchunk, lambda i: mate_copy(0, i).wait_send())
-    each(nchunk, lambda i: mate_copy(1, i).wait_send())
-    each(nchunk, lambda i: far_copy(i).wait_send())
-    each(ndev, lambda k: sq_copy(k).wait_send(), 1)
-    for k in range(1, ngroup):
-        hid_copy(k).wait_send()
-
-    projected = proj_own[...]
-    for k in range(1, ngroup):
-        proj_copy(k).wait_recv()
-        projected = projected + proj_recv[k - 1].astype(jnp.float32)
-    proj_out[...] = projected
-    for k in range(1, ngroup):
-        proj_copy(k).wait_send()
+    factor = jnp.minimum(1.0, norm_limit / jnp.sqrt(jnp.broadcast_to(squares, (1, BLOCK))))
+    factor_one = (1.0 - BETA_ONE) * factor
+    factor_two = (1.0 - BETA_TWO) * factor * factor
+
+    for j in range(nblock):
+        lanes = slice(j * BLOCK, (j + 1) * BLOCK)
+        s = grad_total[:, lanes]
+        one = state_v[0, :, lanes] + factor_one * s
+        two = state_v[1, :, lanes] + factor_two * (s * s)
+        one_out[:, lanes] = one
+        two_out[:, lanes] = two
+        v = two * (1.0 / SECOND_CORR)
+        update = (one * (LEARN_RATE / FIRST_CORR)) / (v * lax.rsqrt(v) + EPSILON)
+        weights_v[:, lanes] = (state_v[2, :, lanes] - update).astype(jnp.bfloat16)
+        partial = jnp.dot(hidden_b[...], weights_v[:, lanes], preferred_element_type=jnp.float32)
+        for k in group_order:
+            proj_send[j, k - 1] = partial[k * tokens : (k + 1) * tokens].astype(jnp.bfloat16)
+        for k in group_order:
+            proj_copy(j, k).start()
+        proj_own[:, lanes] = partial[0:tokens]
+
+    drain(squares_all.at[pl.ds(1, ndev - 1)], sq_send_sem)
+    for j in range(nblock):
+        lanes = slice(j * BLOCK, (j + 1) * BLOCK)
+        projected = proj_own[:, lanes]
+        drain(proj_recv.at[j], proj_recv_sem.at[j])
+        for k in range(1, ngroup):
+            projected = projected + proj_recv[j, k - 1].astype(jnp.float32)
+        proj_out[:, lanes] = projected
+    drain(proj_send, proj_send_sem)
 
 
 def finish_kernel(
@@ -521,7 +559,7 @@
     nrow, nstep, width = hidden_in.shape
     tokens = nrow * nstep
     heads = cols // (2 * HD)
-    nchunk = rows // CHUNK
+    plan = chunk_plan(rows)
     f32, bf16 = jnp.float32, jnp.bfloat16
     vm = pltpu.VMEM
     dma = pltpu.SemaphoreType.DMA
@@ -538,42 +576,30 @@
         scratch_shapes=[
             pltpu.SMEM((nrow,), jnp.int32),
             vm(queries.shape, bf16),
-            vm((rows, cols), f32),
-            vm((rows, cols), f32),
-            vm((rows, cols), f32),
-            vm((rows, cols), f32),
+            vm((sum(n for _, n in plan[:EARLY]), cols), f32),
+            vm((2 * rows, cols), f32),
             vm((rows, cols), bf16),
             vm((rows, cols), bf16),
+            vm((2, rows, cols), f32),
             vm((rows, cols), f32),
-            vm((rows, cols), f32),
-            vm((rows, cols), f32),
-            vm((rows, cols), f32),
-            vm(cache_keys.shape, bf16),
-            vm(cache_values.shape, bf16),
+            vm((3, rows, cols), f32),
+            vm((nrow, 2) + cache_keys.shape[1:], bf16),
             vm((ngroup, nrow, nstep, rows), bf16),
             vm((ngroup * tokens, rows), f32),
+            vm((ngroup * tokens, rows), bf16),
             vm((rows, cols), bf16),
             vm((1, 128), f32),
             vm((ndev, 1, 128), f32),
             vm((tokens, cols), f32),
-            vm((ngroup - 1, tokens, cols), bf16),
-            vm((ngroup - 1, tokens, cols), bf16),
-            dma((2, nchunk)),
-            dma((2, nchunk)),
-            dma((2, nchunk)),
-            dma((nchunk,)),
-            dma((nchunk,)),
-            dma((ngroup - 1,)),
-            dma((ngroup - 1,)),
-            dma((ndev,)),
-            dma((ndev,)),
-            dma((ngroup - 1,)),
-            dma((ngroup - 1,)),
-            dma((3,)),
-            dma((2, nrow)),
-            dma((3,)),
-            pltpu.SemaphoreType.REGULAR((ndev.bit_length() - 1,)),
-        ],
+            vm((cols // BLOCK, ngroup - 1, tokens, BLOCK), bf16),
+            vm((cols // BLOCK, ngroup - 1, tokens, BLOCK), bf16),
+            dma((len(plan),)),
+            dma((len(plan),)),
+            dma((cols // BLOCK,)),
+            dma((nrow,)),
+        ]
+        + [pltpu.SemaphoreType.DMA] * 13
+        + [pltpu.SemaphoreType.REGULAR((ndev.bit_length() - 1,))],
         compiler_params=pltpu.CompilerParams(
             collective_id=0, has_side_effects=True, vmem_limit_bytes=60 * 1024 * 1024 + 320 * 1024
         ),

time: 37.9 us -> 35 us (0.923)
  Pallas kernels: 37.1 us -> 34.2 us
    pallas_call x1, Pallas kernels: 35 us -> 32.1 us  [fused_body(): pl.pallas_call(functools.partial(fused_kernel, sizes), out_shape=(moment,...]
where the time goes in v1:
time: 35 us; the launch traced here: 34.9 us
  Pallas kernels  34.2 us (98%)
  between operations  0.64 us (2%)
    pallas_call x1, Pallas kernels, fused_body(): pl.pallas_call(functools.partial(fused_kernel, sizes), out_shape=(moment,...  32.1 us
    pallas_call x1, Pallas kernels, fused_body(): pl.pallas_call(finish_kernel, out_shape=(jax.ShapeDtypeStruct((rows, cols...  2.13 us

profile of v1, /device:TPU:0, one launch (start us, length us, event | category | flops | bytes accessed | tf_op | source)
XLA Modules:
  0.0 34.9 jit_solution(16199968369386368832)
XLA Ops:
  0.6 32.1 %shard_map.120 = (f32[640,512]{1,0:T(8,128)S(1)}, f32[640,512]{1,0:T(8,128)S(1)}, f32[16,512]{1,0:T(8,128)S(1)}, f32[16,128]{1,0:T(8,128)S(1)}, f32[16,128]{1,0:...) custom-call(s32[4]{0:T(128)} %lengths_ref.1, ...), custom_call_target="tpu_custom_call" | custom-call | tf_op jit(solution)/shard_map/pallas_call | solution.py:571
  32.7 2.1 %shard_map.121 = (f32[640,512]{1,0:T(8,128)}, f32[640,512]{1,0:T(8,128)}, bf16[4,4,512]{2,1,0:T(4,128)(2,1)}, bf16[4,4,1280]{2,1,0:T(4,128)(2,1)}) custom-call(f32[640,512]{1,0:T(8,128)S(1)} %get-tuple-element.13.one_ref, f32[640,512]{1,0:T(8,128)S(1)} %get-tuple-element.14.two_ref, f32[16,512]{1,0:T(8,128)S(1)} %get-tuple-element.15.proj_ref, ...), custom_call_target="tpu_custom_call" | custom-call | tf_op jit(solution)/shard_map/pallas_call | solution.py:607

commit v2 on v1

--- a/solution.py
+++ b/solution.py
@@ -120,12 +120,14 @@
 
 MESH = pl.DeviceIdType.MESH
 PAD = 32
-BLOCK = 128
-EARLY = 2
+BLOCK = 256
+DIRECT = 64
+STEP_SIZE = LEARN_RATE / FIRST_CORR * math.sqrt(SECOND_CORR)
+STEP_EPSILON = EPSILON * math.sqrt(SECOND_CORR)
 
 
 def chunk_plan(rows):
-    sizes = [32, 64]
+    sizes = [DIRECT // 2, DIRECT // 2, DIRECT // 2, DIRECT // 2, 64]
     left = rows - sum(sizes) - 32
     while left > 0:
         sizes.append(min(96, left))
@@ -157,17 +159,21 @@
     lengths_s,
     queries_v,
     mate_src,
+    direct_src,
+    direct_send,
+    direct_in,
     fwd_in,
     fwd_send,
     sum_far,
     sum_in,
     grad_total,
+    grad_square,
+    step_v,
     state_v,
     cache_v,
     hidden_in_v,
     hidden_f,
     hidden_b,
-    weights_v,
     squares_send,
     squares_all,
     proj_own,
@@ -176,21 +182,24 @@
     fwd_sem,
     far_recv_sem,
     proj_recv_sem,
+    sum_sem,
+    direct_recv_sem,
+    hid_recv_sem,
+    sq_recv_sem,
+    round_sem,
     cache_sem,
-    sum_sem,
     early_sem,
+    first_sem,
+    direct_send_sem,
     mate_send_sem,
     far_send_sem,
     hid_send_sem,
-    hid_recv_sem,
     sq_send_sem,
-    sq_recv_sem,
     proj_send_sem,
     load_sem,
     length_sem,
     query_sem,
     own_sem,
-    round_sem,
 ):
     ngrp, nrep, ntp = sizes
     ngroup = ngrp * nrep
@@ -252,6 +261,7 @@
 
     for b in range(bits):
         pl.semaphore_signal(barrier, inc=1, device_id=across(b), device_id_type=MESH)
+    pl.semaphore_signal(barrier, inc=1, device_id=peer(tp=3), device_id_type=MESH)
 
     def block(start, n, owner):
         return grad_ref.at[0, pl.ds(start, n), pl.ds(pl.multiple_of(owner * cols, cols), cols)]
@@ -259,9 +269,32 @@
     def drain(ref, sem):
         pltpu.make_async_copy(ref, ref, sem).wait()
 
-    early = sum(n for _, n in plan[:EARLY])
-    early_copy = pltpu.make_async_copy(block(0, early, far_mate), mate_src, early_sem)
+    target = (1 - y) * 2
+    direct_copy = pltpu.make_async_copy(block(0, DIRECT, target), direct_src, first_sem)
+    early_start = pl.multiple_of(c * DIRECT, DIRECT)
+    early_copy = pltpu.make_async_copy(block(early_start, DIRECT, far_mate), mate_src, early_sem)
     early_copy.start()
+    direct_copy.start()
+
+    direct_put = pltpu.make_async_remote_copy(
+        src_ref=direct_send,
+        dst_ref=direct_in.at[c],
+        send_sem=direct_send_sem,
+        recv_sem=direct_recv_sem,
+        device_id={**base, "tp": target},
+        device_id_type=MESH,
+    )
+
+    def early_mate(i):
+        half = DIRECT // 2
+        return pltpu.make_async_remote_copy(
+            src_ref=mate_src.at[pl.ds(i * half, half)],
+            dst_ref=fwd_in.at[pl.ds(pl.multiple_of(2 * (early_start + i * half) + half, half), half)],
+            send_sem=mate_send_sem,
+            recv_sem=fwd_sem.at[2 * c + i],
+            device_id=peer(tp=1),
+            device_id_type=MESH,
+        )
 
     def own_copy(i):
         start, n = plan[i]
@@ -270,7 +303,7 @@
     def mate_copy(i):
         start, n = plan[i]
         return pltpu.make_async_remote_copy(
-            src_ref=mate_src.at[pl.ds(start, n)] if i < EARLY else block(start, n, far_mate),
+            src_ref=block(start, n, far_mate),
             dst_ref=fwd_in.at[pl.ds(2 * start + n, n)],
             send_sem=mate_send_sem,
             recv_sem=fwd_sem.at[i],
@@ -321,20 +354,35 @@
             device_id_type=MESH,
         )
 
-    for i in range(nchunk):
-        own_copy(i).start()
     length_copy = pltpu.make_async_copy(lengths_ref, lengths_s, length_sem)
     query_copy = pltpu.make_async_copy(queries_ref, queries_v, query_sem)
     own_hidden = pltpu.make_async_copy(
         hidden_ref.at[:, :, pl.ds(pl.multiple_of(p * rows, 128), rows)], hidden_in_v.at[0], own_sem
     )
-    for copy in (length_copy, query_copy, own_hidden):
-        copy.start()
 
     early_copy.wait()
-    pl.semaphore_wait(barrier, bits)
-
-    for i in range(nchunk):
+    pl.semaphore_wait(barrier, bits + 1)
+
+    early_mate(0).start()
+    early_mate(1).start()
+    direct_copy.wait()
+    direct_send[...] = direct_src[...].astype(jnp.bfloat16)
+    direct_put.start()
+
+    @pl.when(c == 1)
+    def _():
+        own_copy(0).start()
+        own_copy(1).start()
+
+    for i in range(2, nchunk):
+        own_copy(i).start()
+
+    @pl.when(c == 0)
+    def _():
+        mate_copy(2).start()
+        mate_copy(3).start()
+
+    for i in range(4, nchunk):
         mate_copy(i).start()
     pltpu.make_async_remote_copy(
         src_ref=block(0, rows, mate),
@@ -344,6 +392,8 @@
         device_id=peer(tp=1),
         device_id_type=MESH,
     ).start()
+    for copy in (length_copy, query_copy, own_hidden):
+        copy.start()
     for i in range(nrow):
         pltpu.make_async_copy(keys_ref.at[i], cache_v.at[i, 0], cache_sem.at[i]).start()
         pltpu.make_async_copy(values_ref.at[i], cache_v.at[i, 1], cache_sem.at[i]).start()
@@ -362,7 +412,10 @@
     for b in range(bits):
         pl.semaphore_signal(round_sem.at[b], inc=1, device_id=across(b), device_id_type=MESH)
         for i in range(b * nchunk // bits, (b + 1) * nchunk // bits):
-            forward(i)
+            if i < 2:
+                pl.when(c == 1)(functools.partial(forward, i))
+            else:
+                forward(i)
         pl.semaphore_wait(round_sem.at[b], 1)
     for k in group_order:
         hid_copy(k).start()
@@ -413,7 +466,7 @@
 
     def prescale(i, carry):
         here = pl.ds(pl.multiple_of(i * 64, 64), 64)
-        state_v[0, here, :] = BETA_ONE * state_v[0, here, :]
+        step_v[here, :] = (BETA_ONE * STEP_SIZE) * state_v[0, here, :]
         state_v[1, here, :] = BETA_TWO * state_v[1, here, :]
         return carry
 
@@ -429,44 +482,75 @@
     hidden_b[...] = hidden_f[...].astype(jnp.bfloat16)
 
     drain(sum_in, sum_sem)
+
+    @pl.when(c == 0)
+    def _():
+        drain(direct_in, direct_recv_sem)
+        sum_in[0, :DIRECT, :] = (
+            sum_in[0, :DIRECT, :] + direct_in[0].astype(jnp.float32) + direct_in[1].astype(jnp.float32)
+        )
+        sum_far[:DIRECT, :] = jnp.zeros((DIRECT, cols), jnp.bfloat16)
+
+    @pl.when(c == 1)
+    def _():
+        for i in range(2):
+            start, n = plan[i]
+            drain(sum_far.at[pl.ds(start, n)], far_recv_sem.at[i])
+
     acc = jnp.zeros((8, cols), jnp.float32)
     for i, (start, n) in enumerate(plan):
         here = slice(start, start + n)
-        drain(sum_far.at[pl.ds(start, n)], far_recv_sem.at[i])
+        if i > 1:
+            drain(sum_far.at[pl.ds(start, n)], far_recv_sem.at[i])
         s = sum_in[0, here, :] + sum_in[1, here, :] + sum_far[here, :].astype(jnp.float32)
         grad_total[here, :] = s
-        acc = acc + jnp.sum((s * s).reshape(n // 8, 8, cols), axis=0)
+        square = s * s
+        grad_square[here, :] = square
+        acc = acc + jnp.sum(square.reshape(n // 8, 8, cols), axis=0)
     mine = jnp.sum(sum(acc[:, j * 128 : (j + 1) * 128] for j in range(cols // 128)), axis=0, keepdims=True)
     squares_send[...] = mine
     for k in flat_order:
         sq_copy(k).start()
     squares_all[0] = mine
-    drain(fwd_in, mate_send_sem)
-    drain(fwd_send, far_send_sem)
+    drain(direct_send, direct_send_sem)
+
+    @pl.when(c == 0)
+    def _():
+        drain(fwd_in, mate_send_sem)
+        drain(fwd_send.at[pl.ds(DIRECT, rows - DIRECT)], far_send_sem)
+
+    @pl.when(c == 1)
+    def _():
+        drain(fwd_in.at[pl.ds(DIRECT, 2 * rows - DIRECT)], mate_send_sem)
+        drain(fwd_send, far_send_sem)
+
     drain(hidden_in_v.at[pl.ds(1, ngroup - 1)], hid_send_sem)
     drain(squares_all.at[pl.ds(1, ndev - 1)], sq_recv_sem)
     squares = jnp.sum(jnp.sum(squares_all[...], axis=0), axis=1, keepdims=True)
     norm_limit = math.sqrt(D * 2 * KVH * HD)
     factor = jnp.minimum(1.0, norm_limit / jnp.sqrt(jnp.broadcast_to(squares, (1, BLOCK))))
-    factor_one = (1.0 - BETA_ONE) * factor
+    factor_step = ((1.0 - BETA_ONE) * STEP_SIZE) * factor
     factor_two = (1.0 - BETA_TWO) * factor * factor
+
+    def weights(lanes):
+        step = step_v[:, lanes] + factor_step * grad_total[:, lanes]
+        two = state_v[1, :, lanes] + factor_two * grad_square[:, lanes]
+        return (state_v[2, :, lanes] - step / (two * lax.rsqrt(two) + STEP_EPSILON)).astype(jnp.bfloat16)
 
     for j in range(nblock):
         lanes = slice(j * BLOCK, (j + 1) * BLOCK)
-        s = grad_total[:, lanes]
-        one = state_v[0, :, lanes] + factor_one * s
-        two = state_v[1, :, lanes] + factor_two * (s * s)
-        one_out[:, lanes] = one
-        two_out[:, lanes] = two
-        v = two * (1.0 / SECOND_CORR)
-        update = (one * (LEARN_RATE / FIRST_CORR)) / (v * lax.rsqrt(v) + EPSILON)
-        weights_v[:, lanes] = (state_v[2, :, lanes] - update).astype(jnp.bfloat16)
-        partial = jnp.dot(hidden_b[...], weights_v[:, lanes], preferred_element_type=jnp.float32)
+        partial = jnp.dot(hidden_b[...], weights(lanes), preferred_element_type=jnp.float32)
         for k in group_order:
             proj_send[j, k - 1] = partial[k * tokens : (k + 1) * tokens].astype(jnp.bfloat16)
         for k in group_order:
             proj_copy(j, k).start()
         proj_own[:, lanes] = partial[0:tokens]
+
+    factor_one = (1.0 - BETA_ONE) * factor
+    for j in range(nblock):
+        lanes = slice(j * BLOCK, (j + 1) * BLOCK)
+        one_out[:, lanes] = BETA_ONE * state_v[0, :, lanes] + factor_one * grad_total[:, lanes]
+        two_out[:, lanes] = state_v[1, :, lanes] + factor_two * grad_square[:, lanes]
 
     drain(squares_all.at[pl.ds(1, ndev - 1)], sq_send_sem)
     for j in range(nblock):
@@ -494,14 +578,19 @@
     entries_out,
     attended_out,
     heads_v,
-    out_sem,
+    entries_v,
+    attended_v,
+    one_sem,
+    two_sem,
+    entries_sem,
+    attended_sem,
 ):
-    outs = [
-        pltpu.make_async_copy(one_ref, one_out, out_sem.at[0]),
-        pltpu.make_async_copy(two_ref, two_out, out_sem.at[1]),
-    ]
-    for copy in outs:
-        copy.start()
+    rows = one_ref.shape[0]
+    part = rows // 5
+    for src, dst, sem in ((one_ref, one_out, one_sem), (two_ref, two_out, two_sem)):
+        for i in range(5):
+            here = pl.ds(i * part, part)
+            pltpu.make_async_copy(src.at[here], dst.at[here], sem).start()
     nrow, nstep, cols = entries_out.shape
     tokens = nrow * nstep
     heads = cols // (2 * HD)
@@ -510,18 +599,21 @@
     qi = lax.broadcasted_iota(jnp.int32, (nrow * PAD, tokens), 0)
     kj = lax.broadcasted_iota(jnp.int32, (nrow * PAD, tokens), 1)
     seen = (qi // PAD == kj // nstep) & (qi % nstep >= kj % nstep)
+    new_keys, new_values = [], []
     for a in range(heads):
         k = proj_ref[:, 2 * a * HD : (2 * a + 1) * HD]
         k = k * cos_ref[...] + pltpu.roll(k, HD // 2, 1) * sin_ref[...]
         v = proj_ref[:, (2 * a + 1) * HD : (2 * a + 2) * HD]
-        new_k = k.astype(jnp.bfloat16)
-        new_v = v.astype(jnp.bfloat16)
+        new_keys.append(k.astype(jnp.bfloat16))
+        new_values.append(v.astype(jnp.bfloat16))
         for i in range(nrow):
             rows_i = slice(i * nstep, (i + 1) * nstep)
-            entries_out[i, :, 2 * a * HD : (2 * a + 1) * HD] = k[rows_i].astype(jnp.bfloat16)
-            entries_out[i, :, (2 * a + 1) * HD : (2 * a + 2) * HD] = v[rows_i].astype(jnp.bfloat16)
+            entries_v[i, :, 2 * a * HD : (2 * a + 1) * HD] = k[rows_i].astype(jnp.bfloat16)
+            entries_v[i, :, (2 * a + 1) * HD : (2 * a + 2) * HD] = v[rows_i].astype(jnp.bfloat16)
+    pltpu.make_async_copy(entries_v, entries_out, entries_sem).start()
+    for a in range(heads):
         scores = lax.dot_general(
-            query_ref[a].astype(jnp.bfloat16), new_k, (((1,), (1,)), ((), ())), preferred_element_type=jnp.float32
+            query_ref[a].astype(jnp.bfloat16), new_keys[a], (((1,), (1,)), ((), ())), preferred_element_type=jnp.float32
         )
         scores = jnp.where(seen, scores * scaling, NEG_FILL)
         before = max_ref[a][:, 0:1]
@@ -529,15 +621,21 @@
         alpha = jnp.exp(before - top)
         e = jnp.exp(scores - top)
         whole = sum_ref[a][:, 0:1] * alpha + jnp.sum(e, -1, keepdims=True)
-        o = old_ref[a] * alpha + jnp.dot(e.astype(jnp.bfloat16), new_v, preferred_element_type=jnp.float32)
+        o = old_ref[a] * alpha + jnp.dot(e.astype(jnp.bfloat16), new_values[a], preferred_element_type=jnp.float32)
         heads_v[a] = o / whole
         for i in range(nrow):
             for j in range(groups):
                 n = a * groups + j
                 at = i * PAD + j * nstep
-                attended_out[i, :, n * HD : (n + 1) * HD] = heads_v[a, at : at + nstep, :].astype(jnp.bfloat16)
-    for copy in outs:
-        copy.wait()
+                attended_v[i, :, n * HD : (n + 1) * HD] = heads_v[a, at : at + nstep, :].astype(jnp.bfloat16)
+    pltpu.make_async_copy(attended_v, attended_out, attended_sem).start()
+    for src, dst, sem in (
+        (one_ref, one_out, one_sem),
+        (two_ref, two_out, two_sem),
+        (entries_v, entries_out, entries_sem),
+        (attended_v, attended_out, attended_sem),
+    ):
+        pltpu.make_async_copy(src, dst, sem).wait()
 
 
 def fused_body(
@@ -568,26 +666,37 @@
     per_head = vm((heads, nrow * PAD, HD), f32)
     moment = vm((rows, cols), f32)
     table = vm((tokens, HD), f32)
+
+    def with_local(*refs):
+        def inner(*local):
+            fused_kernel(sizes, *refs, *local)
+
+        pl.run_scoped(inner, dma((nrow,)), *[pltpu.SemaphoreType.DMA] * 12)
+
     middle = pl.pallas_call(
-        functools.partial(fused_kernel, sizes),
+        with_local,
         out_shape=(moment, moment, vm((tokens, cols), f32), table, table) + (per_head,) * 4,
         in_specs=[hbm] * 9,
         out_specs=(vmem,) * 9,
         scratch_shapes=[
             pltpu.SMEM((nrow,), jnp.int32),
             vm(queries.shape, bf16),
-            vm((sum(n for _, n in plan[:EARLY]), cols), f32),
+            vm((DIRECT, cols), f32),
+            vm((DIRECT, cols), f32),
+            vm((DIRECT, cols), bf16),
+            vm((2, DIRECT, cols), bf16),
             vm((2 * rows, cols), f32),
             vm((rows, cols), bf16),
             vm((rows, cols), bf16),
             vm((2, rows, cols), f32),
+            vm((rows, cols), f32),
+            vm((rows, cols), f32),
             vm((rows, cols), f32),
             vm((3, rows, cols), f32),
             vm((nrow, 2) + cache_keys.shape[1:], bf16),
             vm((ngroup, nrow, nstep, rows), bf16),
             vm((ngroup * tokens, rows), f32),
             vm((ngroup * tokens, rows), bf16),
-            vm((rows, cols), bf16),
             vm((1, 128), f32),
             vm((ndev, 1, 128), f32),
             vm((tokens, cols), f32),
@@ -596,9 +705,8 @@
             dma((len(plan),)),
             dma((len(plan),)),
             dma((cols // BLOCK,)),
-            dma((nrow,)),
         ]
-        + [pltpu.SemaphoreType.DMA] * 13
+        + [pltpu.SemaphoreType.DMA] * 4
         + [pltpu.SemaphoreType.REGULAR((ndev.bit_length() - 1,))],
         compiler_params=pltpu.CompilerParams(
             collective_id=0, has_side_effects=True, vmem_limit_bytes=60 * 1024 * 1024 + 320 * 1024
@@ -613,8 +721,9 @@
             jax.ShapeDtypeStruct(queries.shape, bf16),
         ),
         in_specs=[vmem] * 9,
-        out_specs=(hbm, hbm, vmem, vmem),
-        scratch_shapes=[vm((heads, nrow * PAD, HD), f32), dma((2,))],
+        out_specs=(hbm,) * 4,
+        scratch_shapes=[vm((heads, nrow * PAD, HD), f32), vm((nrow, nstep, cols), bf16), vm(queries.shape, bf16)]
+        + [pltpu.SemaphoreType.DMA] * 4,
         compiler_params=pltpu.CompilerParams(vmem_limit_bytes=8 * 1024 * 1024),
     )(*middle)
 

time: 35 us -> 33.3 us (0.951)
  Pallas kernels: 34.2 us -> 32.5 us
    pallas_call x1, Pallas kernels: 32.1 us -> 31 us  [fused_body(): pl.pallas_call(with_local, out_shape=(moment, moment, vm((tokens, cols),...]
    pallas_call x1, Pallas kernels: 2.13 us -> 1.55 us  [fused_body(): pl.pallas_call(finish_kernel, out_shape=(jax.ShapeDtypeStruct((rows, cols...]
where the time goes in v2:
time: 33.3 us; the launch traced here: 33.2 us
  Pallas kernels  32.5 us (98%)
  between operations  0.64 us (2%)
    pallas_call x1, Pallas kernels, fused_body(): pl.pallas_call(with_local, out_shape=(moment, moment, vm((tokens, cols),...  31 us
    pallas_call x1, Pallas kernels, fused_body(): pl.pallas_call(finish_kernel, out_shape=(jax.ShapeDtypeStruct((rows, cols...  1.55 us

profile of v2, /device:TPU:0, one launch (start us, length us, event | category | flops | bytes accessed | tf_op | source)
XLA Modules:
  0.0 33.2 jit_solution(13684994128424110630)
XLA Ops:
  0.6 31.0 %shard_map.120 = (f32[640,512]{1,0:T(8,128)S(1)}, f32[640,512]{1,0:T(8,128)S(1)}, f32[16,512]{1,0:T(8,128)S(1)}, f32[16,128]{1,0:T(8,128)S(1)}, f32[16,128]{1,0:...) custom-call(s32[4]{0:T(128)} %refs_0_.1, ...), custom_call_target="tpu_custom_call" | custom-call | tf_op jit(solution)/shard_map/pallas_call | solution.py:676
  31.6 1.5 %shard_map.121 = (f32[640,512]{1,0:T(8,128)}, f32[640,512]{1,0:T(8,128)}, bf16[4,4,512]{2,1,0:T(4,128)(2,1)}, bf16[4,4,1280]{2,1,0:T(4,128)(2,1)}) custom-call(f32[640,512]{1,0:T(8,128)S(1)} %get-tuple-element.13.one_ref, f32[640,512]{1,0:T(8,128)S(1)} %get-tuple-element.14.two_ref, f32[16,512]{1,0:T(8,128)S(1)} %get-tuple-element.15.proj_ref, ...), custom_call_target="tpu_custom_call" | custom-call | tf_op jit(solution)/shard_map/pallas_call | solution.py:715

commit v3 on v2

--- a/solution.py
+++ b/solution.py
@@ -130,7 +130,7 @@
     sizes = [DIRECT // 2, DIRECT // 2, DIRECT // 2, DIRECT // 2, 64]
     left = rows - sum(sizes) - 32
     while left > 0:
-        sizes.append(min(96, left))
+        sizes.append(min(192, left))
         left -= sizes[-1]
     sizes.append(32)
     return [(sum(sizes[:i]), n) for i, n in enumerate(sizes)]
@@ -169,6 +169,8 @@
     grad_total,
     grad_square,
     step_v,
+    share_v,
+    share_square,
     state_v,
     cache_v,
     hidden_in_v,
@@ -179,6 +181,7 @@
     proj_own,
     proj_send,
     proj_recv,
+    proj_count,
     fwd_sem,
     far_recv_sem,
     proj_recv_sem,
@@ -186,6 +189,7 @@
     direct_recv_sem,
     hid_recv_sem,
     sq_recv_sem,
+    share_recv_sem,
     round_sem,
     cache_sem,
     early_sem,
@@ -200,6 +204,7 @@
     length_sem,
     query_sem,
     own_sem,
+    share_send_sem,
 ):
     ngrp, nrep, ntp = sizes
     ngroup = ngrp * nrep
@@ -344,13 +349,24 @@
             device_id_type=MESH,
         )
 
-    def proj_copy(j, k):
+    def proj_copy(j, k, shared=False):
         return pltpu.make_async_remote_copy(
-            src_ref=proj_send.at[j, k - 1],
-            dst_ref=proj_recv.at[j, k - 1],
+            src_ref=proj_send.at[nblock if shared else j, k],
+            dst_ref=proj_recv.at[j, k],
             send_sem=proj_send_sem,
             recv_sem=proj_recv_sem.at[j],
-            device_id=group_peer(k),
+            device_id=peer(tp=1, **group_bits(k)) if shared else group_peer(k),
+            device_id_type=MESH,
+        )
+
+    def share_copy(i):
+        src = (one_ref, two_ref, master_ref, grad_total)[i]
+        return pltpu.make_async_remote_copy(
+            src_ref=src.at[:, pl.ds(0, BLOCK)],
+            dst_ref=share_v.at[i],
+            send_sem=share_send_sem,
+            recv_sem=share_recv_sem,
+            device_id=peer(tp=1),
             device_id_type=MESH,
         )
 
@@ -392,6 +408,12 @@
         device_id=peer(tp=1),
         device_id_type=MESH,
     ).start()
+
+    @pl.when(c == 0)
+    def _():
+        for i in range(3):
+            share_copy(i).start()
+
     for copy in (length_copy, query_copy, own_hidden):
         copy.start()
     for i in range(nrow):
@@ -512,6 +534,24 @@
     for k in flat_order:
         sq_copy(k).start()
     squares_all[0] = mine
+
+    @pl.when(c == 0)
+    def _():
+        share_copy(3).start()
+
+    @pl.when(c == 1)
+    def _():
+        drain(share_v, share_recv_sem)
+
+        def prepare(i, carry):
+            here = pl.ds(pl.multiple_of(i * 64, 64), 64)
+            share_v[0, here, :] = (BETA_ONE * STEP_SIZE) * share_v[0, here, :]
+            share_v[1, here, :] = BETA_TWO * share_v[1, here, :]
+            share_square[here, :] = share_v[3, here, :] * share_v[3, here, :]
+            return carry
+
+        lax.fori_loop(0, rows // 64, prepare, 0)
+
     drain(direct_send, direct_send_sem)
 
     @pl.when(c == 0)
@@ -532,19 +572,44 @@
     factor_step = ((1.0 - BETA_ONE) * STEP_SIZE) * factor
     factor_two = (1.0 - BETA_TWO) * factor * factor
 
-    def weights(lanes):
-        step = step_v[:, lanes] + factor_step * grad_total[:, lanes]
-        two = state_v[1, :, lanes] + factor_two * grad_square[:, lanes]
-        return (state_v[2, :, lanes] - step / (two * lax.rsqrt(two) + STEP_EPSILON)).astype(jnp.bfloat16)
-
-    for j in range(nblock):
+    def weights(step, two, grad, square, old):
+        step = step + factor_step * grad
+        two = two + factor_two * square
+        return (old - step / (two * lax.rsqrt(two) + STEP_EPSILON)).astype(jnp.bfloat16)
+
+    def project(w):
+        return jnp.dot(hidden_b[...], w, preferred_element_type=jnp.float32)
+
+    def shared_block():
+        partial = project(weights(share_v[0], share_v[1], share_v[3], share_square[...], share_v[2]))
+        for k in group_order + [0]:
+            proj_send[nblock, k] = partial[k * tokens : (k + 1) * tokens].astype(jnp.bfloat16)
+        for k in group_order + [0]:
+            proj_copy(0, k, True).start()
+
+    def block_of(j):
         lanes = slice(j * BLOCK, (j + 1) * BLOCK)
-        partial = jnp.dot(hidden_b[...], weights(lanes), preferred_element_type=jnp.float32)
+        partial = project(
+            weights(
+                step_v[:, lanes], state_v[1, :, lanes], grad_total[:, lanes], grad_square[:, lanes], state_v[2, :, lanes]
+            )
+        )
         for k in group_order:
-            proj_send[j, k - 1] = partial[k * tokens : (k + 1) * tokens].astype(jnp.bfloat16)
+            proj_send[j, k] = partial[k * tokens : (k + 1) * tokens].astype(jnp.bfloat16)
         for k in group_order:
             proj_copy(j, k).start()
         proj_own[:, lanes] = partial[0:tokens]
+
+    @pl.when(c == 1)
+    def _():
+        for j in range(nblock):
+            block_of(j)
+        shared_block()
+
+    @pl.when(c == 0)
+    def _():
+        for j in range(1, nblock):
+            block_of(j)
 
     factor_one = (1.0 - BETA_ONE) * factor
     for j in range(nblock):
@@ -555,12 +620,31 @@
     drain(squares_all.at[pl.ds(1, ndev - 1)], sq_send_sem)
     for j in range(nblock):
         lanes = slice(j * BLOCK, (j + 1) * BLOCK)
+        if j == 0:
+            @pl.when(c == 0)
+            def _():
+                drain(proj_recv.at[0], proj_recv_sem.at[0])
+                proj_own[:, lanes] = proj_recv[0, 0].astype(jnp.float32)
+
+            @pl.when(c == 1)
+            def _():
+                drain(proj_recv.at[0, pl.ds(1, ngroup - 1)], proj_recv_sem.at[0])
+
+        else:
+            drain(proj_recv.at[j, pl.ds(1, ngroup - 1)], proj_recv_sem.at[j])
         projected = proj_own[:, lanes]
-        drain(proj_recv.at[j], proj_recv_sem.at[j])
         for k in range(1, ngroup):
-            projected = projected + proj_recv[j, k - 1].astype(jnp.float32)
+            projected = projected + proj_recv[j, k].astype(jnp.float32)
         proj_out[:, lanes] = projected
-    drain(proj_send, proj_send_sem)
+
+    @pl.when(c == 0)
+    def _():
+        drain(share_v, share_send_sem)
+        drain(proj_recv.at[pl.ds(1, nblock - 1), pl.ds(1, ngroup - 1)], proj_send_sem)
+
+    @pl.when(c == 1)
+    def _():
+        drain(proj_count.at[pl.ds(0, nblock * (ngroup - 1) + ngroup)], proj_send_sem)
 
 
 def finish_kernel(
@@ -671,7 +755,7 @@
         def inner(*local):
             fused_kernel(sizes, *refs, *local)
 
-        pl.run_scoped(inner, dma((nrow,)), *[pltpu.SemaphoreType.DMA] * 12)
+        pl.run_scoped(inner, dma((nrow,)), *[pltpu.SemaphoreType.DMA] * 13)
 
     middle = pl.pallas_call(
         with_local,
@@ -692,6 +776,8 @@
             vm((rows, cols), f32),
             vm((rows, cols), f32),
             vm((rows, cols), f32),
+            vm((4, rows, BLOCK), f32),
+            vm((rows, BLOCK), f32),
             vm((3, rows, cols), f32),
             vm((nrow, 2) + cache_keys.shape[1:], bf16),
             vm((ngroup, nrow, nstep, rows), bf16),
@@ -700,13 +786,14 @@
             vm((1, 128), f32),
             vm((ndev, 1, 128), f32),
             vm((tokens, cols), f32),
-            vm((cols // BLOCK, ngroup - 1, tokens, BLOCK), bf16),
-            vm((cols // BLOCK, ngroup - 1, tokens, BLOCK), bf16),
+            vm((cols // BLOCK + 1, ngroup, tokens, BLOCK), bf16),
+            vm((cols // BLOCK, ngroup, tokens, BLOCK), bf16),
+            vm((cols // BLOCK * (ngroup - 1) + ngroup, tokens, BLOCK), bf16),
             dma((len(plan),)),
             dma((len(plan),)),
             dma((cols // BLOCK,)),
         ]
-        + [pltpu.SemaphoreType.DMA] * 4
+        + [pltpu.SemaphoreType.DMA] * 5
         + [pltpu.SemaphoreType.REGULAR((ndev.bit_length() - 1,))],
         compiler_params=pltpu.CompilerParams(
             collective_id=0, has_side_effects=True, vmem_limit_bytes=60 * 1024 * 1024 + 320 * 1024

time: 33.3 us -> 33.3 us (level)
  no operation moved by 1% of the time
where the time goes in v3:
time: 33.3 us; the launch traced here: 33.2 us
  Pallas kernels  32.5 us (98%)
  between operations  0.64 us (2%)
    pallas_call x1, Pallas kernels, fused_body(): pl.pallas_call(with_local, out_shape=(moment, moment, vm((tokens, cols),...  31 us
    pallas_call x1, Pallas kernels, fused_body(): pl.pallas_call(finish_kernel, out_shape=(jax.ShapeDtypeStruct((rows, cols...  1.55 us

profile of v3, /device:TPU:0, one launch (start us, length us, event | category | flops | bytes accessed | tf_op | source)
XLA Modules:
  0.0 33.2 jit_solution(15929388671882206875)
XLA Ops:
  0.6 31.0 %shard_map.120 = (f32[640,512]{1,0:T(8,128)S(1)}, f32[640,512]{1,0:T(8,128)S(1)}, f32[16,512]{1,0:T(8,128)S(1)}, f32[16,128]{1,0:T(8,128)S(1)}, f32[16,128]{1,0:...) custom-call(s32[4]{0:T(128)} %refs_0_.1, ...), custom_call_target="tpu_custom_call" | custom-call | tf_op jit(solution)/shard_map/pallas_call | solution.py:760
  31.6 1.5 %shard_map.121 = (f32[640,512]{1,0:T(8,128)}, f32[640,512]{1,0:T(8,128)}, bf16[4,4,512]{2,1,0:T(4,128)(2,1)}, bf16[4,4,1280]{2,1,0:T(4,128)(2,1)}) custom-call(f32[640,512]{1,0:T(8,128)S(1)} %get-tuple-element.13.one_ref, f32[640,512]{1,0:T(8,128)S(1)} %get-tuple-element.14.two_ref, f32[16,512]{1,0:T(8,128)S(1)} %get-tuple-element.15.proj_ref, ...), custom_call_target="tpu_custom_call" | custom-call | tf_op jit(solution)/shard_map/pallas_call | solution.py:802
